TPU v7x, 32 devices: a whole 2x2x4 slice. The times are simulated.
32 devices in a mesh: box: 4 (over z), dir: 8 (over y, x, core).
Axes of the slice: x: 2, y: 2, z: 4, core: 2. Of those that a mesh axis runs over, the one named last changes fastest.
Arguments:
- currents: bfloat16 [4096, 256, 128], P(('box', 'dir')), may hold values from -6 to 6
- leaf_parent: int32 [4096], P(('box', 'dir')), may hold values from 0 to 63, as said below
- near_links: int32 [4096, 2], P(('box', 'dir')), may hold values 0 or 1
- near_blocks: bfloat16 [3, 256, 256], replicated, may hold values from -0.375 to 0.375
- aggregate_maps: bfloat16 [64, 256, 256], replicated, may hold values from -0.375 to 0.375
- far_boxes: int32 [64, 64], P('box'), may hold values from 0 to 63
- far_counts: int32 [64], P('box'), may hold values from 16 to 64
- translate_coef: float32 [64, 64, 256], P('box'), may hold values from 0.005 to 0.05
- time_kernel: float32 [128], replicated, may hold values from -0.5 to 0.5
- disaggregate_maps: bfloat16 [64, 256, 256], replicated, may hold values from -0.375 to 0.375
Outputs:
- field: bfloat16 [4096, 256, 128], P(('box', 'dir'))
Inputs may be any that keep to these rules, and one draw needn't show every extreme that they name: `leaf_parent`: the leaves k * 64 to (k + 1) * 64 - 1 share one parent. The leaves g * 1024 to (g + 1) * 1024 - 1 have as parents the top-level boxes g * 16 to (g + 1) * 16 - 1, each exactly once as a run.
All inputs are finite; a program needn't handle non-finite values. No bound on the sum of `near_links` on one device may be relied on, other than what follows from the above.
Results may differ from a plain program's by a relative error of at most 0.0047.
Values may be sent and summed in bfloat16 or wider, within the bound.
A program may use at most 192 MiB of HBM per device.

v0:
```python
import jax
import jax.numpy as jnp
from jax import lax
from jax.sharding import PartitionSpec as P

LEAF_TOP = 64


def with_halo(block, sides, width):
    for axis, dim in sides:
        count = lax.axis_size(axis)
        forward = [(i, i + 1) for i in range(count - 1)]
        backward = [(target, source) for source, target in forward]
        low = lax.ppermute(
            lax.slice_in_dim(block, block.shape[dim] - width, None, axis=dim), axis, forward
        )
        high = lax.ppermute(lax.slice_in_dim(block, 0, width, axis=dim), axis, backward)
        block = jnp.concatenate([low, block, high], axis=dim)
    return block


def time_matrix(kernel):
    length = kernel.shape[0]
    sample_lag = jnp.arange(length)[:, None] - jnp.arange(length)[None, :]
    return jnp.where(
        sample_lag >= 0, kernel[jnp.clip(sample_lag, 0, length - 1)], jnp.zeros((), kernel.dtype)
    )


def per_device(
    currents,
    leaf_parent,
    near_links,
    near_blocks,
    aggregate_maps,
    far_boxes,
    far_counts,
    translate_coef,
    time_kernel,
    disaggregate_maps,
):
    highest = lax.Precision.HIGHEST
    leaf_count, unknowns, samples = currents.shape
    run_length = min(leaf_count, LEAF_TOP)
    run_count = leaf_count // run_length
    top_local, list_slots = far_boxes.shape
    top_total = top_local * lax.axis_size("box")
    direction_total = aggregate_maps.shape[1]
    dir_rows = direction_total // lax.axis_size("dir")
    dir_index = lax.axis_index("dir")
    local_parent = leaf_parent - lax.axis_index("box") * top_local
    run_parent = local_parent.reshape(run_count, run_length)[:, 0]
    run_onehot = (run_parent[:, None] == jnp.arange(top_local)[None, :]).astype(jnp.float32)
    leaf_runs = currents.reshape(run_count, run_length, unknowns, samples)
    map_block = aggregate_maps
    run_sums = jnp.einsum("sqp,bspt->bqt", map_block, leaf_runs, preferred_element_type=jnp.float32)
    own_rays = lax.psum_scatter(
        jnp.einsum("bc,bqt->qct", run_onehot, run_sums, precision=highest),
        "dir",
        scatter_dimension=0,
        tiled=True,
    )
    own_rays = own_rays.astype(jnp.bfloat16)
    is_valid = (jnp.arange(list_slots)[None, :] < far_counts[:, None]).astype(jnp.float32)
    matches = (far_boxes[:, :, None] == jnp.arange(top_total)[None, None, :]).astype(
        jnp.float32
    ) * is_valid[:, :, None]
    coef_block = lax.dynamic_slice_in_dim(translate_coef, dir_index * dir_rows, dir_rows, 2)
    weights = jnp.einsum("cfs,cfq->csq", matches, coef_block, precision=highest)
    far_sum = jnp.einsum(
        "csq,qst->cqt",
        weights,
        lax.all_gather(own_rays, "box", axis=1, tiled=True).astype(jnp.float32),
        precision=highest,
    )
    incoming = jnp.einsum(
        "cqs,ts->cqt", far_sum, time_matrix(time_kernel), precision=highest
    ).astype(jnp.bfloat16)
    selected = jnp.einsum(
        "bc,cqt->bqt",
        run_onehot,
        lax.all_gather(incoming, "dir", axis=1, tiled=True).astype(jnp.float32),
        precision=highest,
    ).astype(jnp.bfloat16)
    map_block = disaggregate_maps
    far_terms = jnp.einsum("spq,bqt->bspt", map_block, selected, preferred_element_type=jnp.float32)
    far_field = far_terms.reshape(leaf_count, unknowns, samples)
    rim_leaves = jnp.concatenate([currents[:1], currents[-1:]], axis=0)
    extended = with_halo(rim_leaves, ((("box", "dir"), 0),), 1)
    link_mask = near_links.astype(jnp.float32)
    self_term = jnp.einsum(
        "pr,lrt->lpt", near_blocks[0], currents, preferred_element_type=jnp.float32
    )
    before_all = jnp.einsum(
        "pr,lrt->lpt", near_blocks[1], currents, preferred_element_type=jnp.float32
    )
    after_all = jnp.einsum(
        "pr,lrt->lpt", near_blocks[2], currents, preferred_element_type=jnp.float32
    )
    before_rim = jnp.dot(near_blocks[1], extended[0], preferred_element_type=jnp.float32)
    after_rim = jnp.dot(near_blocks[2], extended[3], preferred_element_type=jnp.float32)
    before_term = jnp.concatenate([before_rim[None], before_all[:-1]], axis=0)
    after_term = jnp.concatenate([after_all[1:], after_rim[None]], axis=0)
    near_field = (
        self_term
        + link_mask[:, 0, None, None] * before_term
        + link_mask[:, 1, None, None] * after_term
    )
    return (near_field + far_field).astype(jnp.bfloat16)


def solution(mesh):
    return jax.shard_map(
        per_device,
        mesh=mesh,
        in_specs=(
            P(("box", "dir"), None, None),
            P(("box", "dir")),
            P(("box", "dir"), None),
            P(),
            P(),
            P("box", None),
            P("box"),
            P("box", None, None),
            P(),
            P(),
        ),
        out_specs=P(("box", "dir"), None, None),
        check_vma=False,
    )
```

profile of v0, /device:TPU:0, one launch (start us, length us, event | category | flops | bytes accessed | tf_op | source)
XLA Modules:
  0.0 236.6 jit_solution(2107444564521629391)
XLA Ops:
  6.5 0.0 copy-start
  6.5 0.0 reduce-scatter.2.cloned.1.call-start
  6.5 0.0 copy-start.7
  6.5 0.0 copy-start.5
  6.5 8.2 %fusion.8 = f32[2,256,128]{1,2,0:T(8,128)S(1)} fusion(bf16[2,64,256,128]{3,2,1,0:T(8,128)(2,1)} %bitcast.84, bf16[64,256,256]{2,1,0:T(8,128)(2,1)} %param.14), kind=kOutput, calls=%fused_computation.14 | convolution fusion | flops 2147483648 | bytes 17039360 | tf_op jit(solution)/shard_map/sqp,bspt->bqt/dot_general | solution.py:56
  14.8 0.0 copy-start.2
  14.8 0.1 copy.42
  15.0 0.0 copy-done.7
  15.0 0.1 reshape.62
  15.1 0.1 slice_reduce_fusion
  15.2 2.4 %convolution_bitcast_fusion.2 = f32[256,16,128]{2,1,0:T(8,128)} fusion(f32[2,256,128]{2,0,1:T(2,128)S(1)} %copy.42, s32[2]{0:T(128)S(1)} %slice_reduce_fusion), kind=kOutput, calls=%fused_computation.13 | convolution fusion | flops 12582944 | bytes 2359304 | tf_op jit(solution)/shard_map/bc,bqt->qct/dot_general | solution.py:58
  17.6 0.0 reduce-scatter.2.cloned.1.call-update
  17.6 0.0 all-gather.2.cloned.1.call-start
  17.7 0.9 fusion.47
  18.6 2.4 %collective-permute-start = (bf16[1,256,128]{2,1,0:T(8,128)(2,1)S(1)}, bf16[1,256,128]{2,1,0:T(8,128)(2,1)S(1)}, u32[]{:S(2)}, u32[]{:S(2)}) collective-permute-start(bf16[1,256,128]{2,1,0:T(8,128)(2,1)S(1)} %get-tuple-element.6), channel_id=1, source_target_pairs={{0,1},{1,2},{2,3},{3,4},{4,5},{5,6},{6,7},{7,8},{8,9},{9,10},{10,1... | collective-permute-start | bytes 196616 | tf_op jit(solution)/shard_map/ppermute | solution.py:14
  21.0 1.3 collective-permute-start.1
  22.3 0.0 copy-done.5
  22.3 0.0 copy-done.2
  22.4 0.0 copy-start.6
  22.4 0.0 copy-start.4
  22.4 0.0 copy-start.3
  22.4 97.2 %gather_fusion = f32[16384]{0:T(1024)S(1)} fusion(f32[128]{0:T(128)S(1)} %copy-done.2, s32[16384]{0:T(1024)S(1)} %fusion.32), kind=kCustom, calls=%fused_computation | custom fusion | bytes 196608 | tf_op jit(solution)/shard_map/gather | solution.py:26
  119.6 0.0 copy-done.6
  119.6 0.1 fusion.38
  119.7 0.0 copy-done
  119.7 0.0 copy-done.4
  119.7 1.4 fusion.13
  121.1 0.0 reduce-scatter.2.cloned.1.call-done
  121.1 1.0 convert_element_type.27
  122.2 21.0 %all_gather.6 = bf16[32,64,128]{2,0,1:T(8,128)(2,1)S(1)} all-gather(bf16[32,16,128]{2,0,1:T(8,128)(2,1)S(1)} %copy.43), channel_id=1, replica_groups=mesh['box'=4,'dir'=8] {'box'}, dimensions={1}, use_global_device_ids=true | all-gather | bytes 655360 | tf_op jit(solution)/shard_map/all_gather | solution.py:73
  143.1 0.8 convolution_bitcast_fusion.3
  143.9 1.0 convolution_convert_fusion
  145.0 0.0 all-gather.2.cloned.1.call-update
  145.0 0.0 copy-done.3
  145.0 11.5 %convolution_bitcast_fusion.1 = f32[128,256,128]{1,2,0:T(8,128)} fusion(bf16[128,256,128]{2,1,0:T(8,128)(2,1)} %param.10, bf16[3,256,256]{2,1,0:T(8,128)(2,1)S(1)} %copy-done.3), kind=kOutput, calls=%fused_computation.8 | convolution fusion | flops 2147483648 | bytes 25296896 | tf_op jit(solution)/shard_map/pr,lrt->lpt/dot_general | solution.py:94
  156.5 5.8 %convolution_bitcast_fusion = f32[128,256,128]{1,2,0:T(8,128)S(1)} fusion(bf16[128,256,128]{2,1,0:T(8,128)(2,1)} %param.10, bf16[3,256,256]{2,1,0:T(8,128)(2,1)S(1)} %copy-done.3), kind=kOutput, calls=%fused_computation.7 | convolution fusion | flops 2147483648 | bytes 25296896 | tf_op jit(solution)/shard_map/pr,lrt->lpt/dot_general | solution.py:97
  162.3 12.1 %slice.44 = f32[127,256,128]{1,2,0:T(8,128)} slice(f32[128,256,128]{1,2,0:T(8,128)} %convolution_bitcast_fusion.1), slice={[0:127], [0:256], [0:128]} | slice | bytes 33292288 | tf_op jit(solution)/shard_map/slice | solution.py:102
  174.4 6.0 %slice.45 = f32[127,256,128]{1,2,0:T(8,128)} slice(f32[128,256,128]{1,2,0:T(8,128)S(1)} %convolution_bitcast_fusion), slice={[1:128], [0:256], [0:128]} | slice | bytes 33292288 | tf_op jit(solution)/shard_map/slice | solution.py:103
  180.5 0.0 collective-permute-done
  180.5 0.2 convolution_bitcast_fusion.5
  180.7 0.0 collective-permute-done.1
  180.7 0.2 convolution_bitcast_fusion.4
  180.9 0.0 all-gather.2.cloned.1.call-done
  180.9 1.6 fusion.11
  182.5 11.5 %fusion.4 = f32[2,128,64,256]{3,1,2,0:T(8,128)} fusion(bf16[64,256,256]{2,1,0:T(8,128)(2,1)} %param.19, bf16[2,256,128,1]{2,0,1,3:T(2,128)(2,1)S(1)} %fusion.11), kind=kOutput, calls=%fused_computation.9 | convolution fusion | flops 2147483648 | bytes 25296896 | tf_op jit(solution)/shard_map/spq,bqt->bspt/dot_general | solution.py:86
  194.0 0.0 copy-start.1
  194.1 23.8 %fusion.3 = bf16[128,256,128]{1,2,0:T(8,128)(2,1)} fusion(f32[127,256,128]{1,2,0:T(8,128)} %slice.44, f32[1,256,128]{1,2,0:T(8,128)S(1)} %convolution_bitcast_fusion.5, f32[1,256,128]{1,2,0:T(8,128)S(1)} %convolution_bitcast_fusion.4, f32[127,256,128]{1,2,0:T(8,128)} %slice.45, f32[2,128,64,256]{3,1,2,0:T(8,128)} %fusion.4, ...), kind=kOutput, calls=%fused_computation.5 | convolution fusion | flops 2181038080 | bytes 67240960 | tf_op jit(solution)/shard_map/pr,lrt->lpt/dot_general | solution.py:91
  217.8 11.9 %copy.48 = bf16[128,256,128]{2,1,0:T(8,128)(2,1)} copy(bf16[128,256,128]{1,2,0:T(8,128)(2,1)} %fusion.3) | data formatting | bytes 16777216 | tf_op jit(solution)/shard_map/convert_element_type | solution.py:109
  229.7 0.0 copy-done.1
  (5 shorter events, 0.1 us)
Async XLA Ops:
  6.5 113.2 %copy-start = (f32[16,64,256]{2,1,0:T(8,128)S(1)}, f32[16,64,256]{2,1,0:T(8,128)}, u32[]{:S(2)}) copy-start(f32[16,64,256]{2,1,0:T(8,128)} %param.17) | copy-start | bytes 3145732
  6.5 114.6 %reduce-scatter.2.cloned.1.call-start = ((), (), s32[]{:S(2)}) async-start(), calls=%async_computation.1 | async-start | bytes 2359296 | tf_op jit(solution)/shard_map/reduce_scatter | solution.py:57
  6.5 8.4 %copy-start.7 = (s32[128]{0:T(128)S(1)}, s32[128]{0:T(128)}, u32[]{:S(2)}) copy-start(s32[128]{0:T(128)} %param.11) | copy-start | bytes 1540
  6.5 15.7 %copy-start.5 = (s32[128,2]{0,1:T(2,128)S(1)}, s32[128,2]{0,1:T(2,128)}, u32[]{:S(2)}) copy-start(s32[128,2]{0,1:T(2,128)} %param.12) | copy-start | bytes 3076
  14.8 7.5 %copy-start.2 = (f32[128]{0:T(128)S(1)}, f32[128]{0:T(128)}, u32[]{:S(2)}) copy-start(f32[128]{0:T(128)} %param.18) | copy-start | bytes 1540
  17.6 163.3 %all-gather.2.cloned.1.call-start = ((), (), s32[]{:S(2)}) async-start(), calls=%async_computation.2 | async-start | bytes 1179648 | tf_op jit(solution)/shard_map/all_gather | solution.py:82
  18.6 161.9 %collective-permute-start = (bf16[1,256,128]{2,1,0:T(8,128)(2,1)S(1)}, bf16[1,256,128]{2,1,0:T(8,128)(2,1)S(1)}, u32[]{:S(2)}, u32[]{:S(2)}) collective-permute-start(bf16[1,256,128]{2,1,0:T(8,128)(2,1)S(1)} %get-tuple-element.6), channel_id=1, source_target_pairs={{0,1},{1,2},{2,3},{3,4},{4,5},{5,6},{6,7},{7,8},{8,9},{9,10},{10,1... | collective-permute-start | bytes 196616 | tf_op jit(solution)/shard_map/ppermute | solution.py:14
  21.0 159.7 %collective-permute-start.1 = (bf16[1,256,128]{2,1,0:T(8,128)(2,1)S(1)}, bf16[1,256,128]{2,1,0:T(8,128)(2,1)S(1)}, u32[]{:S(2)}, u32[]{:S(2)}) collective-permute-start(bf16[1,256,128]{2,1,0:T(8,128)(2,1)S(1)} %get-tuple-element.5), channel_id=1, source_target_pairs={{1,0},{2,1},{3,2},{4,3},{5,4},{6,5},{7,6},{8,7},{9,8},{10,9},{11,1... | collective-permute-start | bytes 196616 | tf_op jit(solution)/shard_map/ppermute | solution.py:17
  22.4 97.3 %copy-start.6 = (s32[16]{0:T(128)S(1)}, s32[16]{0:T(128)}, u32[]{:S(2)}) copy-start(s32[16]{0:T(128)} %param.16) | copy-start | bytes 196
  22.4 97.3 %copy-start.4 = (s32[16,64]{1,0:T(8,128)S(1)}, s32[16,64]{1,0:T(8,128)}, u32[]{:S(2)}) copy-start(s32[16,64]{1,0:T(8,128)} %param.15) | copy-start | bytes 12292
  22.4 122.6 %copy-start.3 = (bf16[3,256,256]{2,1,0:T(8,128)(2,1)S(1)}, bf16[3,256,256]{2,1,0:T(8,128)(2,1)}, u32[]{:S(2)}) copy-start(bf16[3,256,256]{2,1,0:T(8,128)(2,1)} %param.13) | copy-start | bytes 1179652
  194.0 35.7 %copy-start.1 = (f32[16,64,256]{2,1,0:T(8,128)S(1)}, f32[16,64,256]{2,1,0:T(8,128)}, u32[]{:S(2)}) copy-start(f32[16,64,256]{2,1,0:T(8,128)} %param.17) | copy-start | bytes 3145732
Sparse Core Ops, SparseCore 0:
  17.8 43.8 reduce-scatter.1
  145.1 23.1 all-gather.1
where the time goes:
time: 237 us
  local copies, waits for them, and re-layouts  129 us (54%)
  matrix products  68.5 us (29%)
  blocking collectives  21 us (9%)
  between operations  13.6 us (6%)
  starting transfers between devices  3.74 us (2%)
    gather x1, local copies, waits for them, and re-layouts, time_matrix(): kernel[jnp.clip(sample_lag, 0, length - 1)]  97.2 us
    dot_general x1, matrix products, per_device(): jnp.einsum('pr,lrt->lpt', near_blocks[0], currents, preferred_element_typ...  23.8 us
    all_gather x1, blocking collectives, per_device(): lax.all_gather(own_rays, 'box', axis=1, tiled=True).astype(jnp.float32)  21 us
    slice x1, local copies, waits for them, and re-layouts, per_device(): before_term = jnp.concatenate([before_rim[None], before_all[:-1]], axis=0)  12.1 us
    convert_element_type x1, local copies, waits for them, and re-layouts, per_device(): return (near_field + far_field).astype(jnp.bfloat16)  11.9 us
    dot_general x1, matrix products, per_device(): jnp.einsum('spq,bqt->bspt', map_block, selected, preferred_element_type=j...  11.5 us
    dot_general x1, matrix products, per_device(): jnp.einsum('pr,lrt->lpt', near_blocks[1], currents, preferred_element_typ...  11.5 us
    dot_general x1, matrix products, per_device(): jnp.einsum('sqp,bspt->bqt', map_block, leaf_runs, preferred_element_type=...  8.24 us
  transfers between devices with their start and end apart: 4, of which 0 were waited for; matrix products, arithmetic and copies ran while one was open for 58% of the time, Pallas kernels for 0%

commit v1 on v0

v1 whole, which is shorter than its diff:
```python
import functools
import jax
import jax.numpy as jnp
from jax import lax
from jax.experimental import pallas as pl
from jax.experimental.pallas import tpu as pltpu
from jax.sharding import PartitionSpec as P

LEAF_TOP = 64
MESH = pl.DeviceIdType.MESH
HIGHEST = lax.Precision.HIGHEST


def aggregate_kernel(runs, chunk, maps_ref, cur_ref, out_ref, acc_ref):
    step = pl.program_id(0)
    samples = cur_ref.shape[-1]

    @pl.when(step == 0)
    def _():
        acc_ref[...] = jnp.zeros_like(acc_ref)

    total = acc_ref[...]
    for i in range(chunk):
        pair = jnp.concatenate([cur_ref[j, i] for j in range(runs)], axis=1)
        total = total + jnp.dot(maps_ref[i], pair, preferred_element_type=jnp.float32)
    acc_ref[...] = total

    @pl.when(step == pl.num_programs(0) - 1)
    def _():
        for j in range(runs):
            out_ref[j] = acc_ref[:, j * samples : (j + 1) * samples].astype(jnp.bfloat16)


def translate_kernel(
    boxes,
    dirs,
    runs,
    top_local,
    rays_ref,
    parent_ref,
    lists_ref,
    coef_ref,
    kernel_ref,
    out_ref,
    rays_all,
    parent_all,
    weights_ref,
    far_ref,
    stage_ref,
    landed,
    ray_send,
    ray_recv,
    par_send,
    par_recv,
    back_send,
    back_recv,
):
    my_box = lax.axis_index("box")
    my_dir = lax.axis_index("dir")
    me = my_box * dirs + my_dir
    rows = coef_ref.shape[1]
    samples = rays_ref.shape[-1]
    peers = [(kb, kd) for kb in range(boxes) for kd in range(dirs) if kb or kd]
    peers.sort(key=lambda p: -min(p[0], boxes - p[0]))

    def target(kb, kd):
        return lax.rem(my_box + kb, boxes), lax.rem(my_dir + kd, dirs)

    barrier = pltpu.get_barrier_semaphore()
    for kb, kd in peers:
        tb, td = target(kb, kd)
        pl.semaphore_signal(
            barrier, inc=1, device_id={"box": tb, "dir": td}, device_id_type=MESH
        )
    pl.semaphore_wait(barrier, len(peers))

    def parent_copy(kb, kd):
        tb, td = target(kb, kd)
        return pltpu.make_async_remote_copy(
            src_ref=parent_ref,
            dst_ref=parent_all.at[me],
            send_sem=par_send.at[tb * dirs + td],
            recv_sem=par_recv.at[me],
            device_id={"box": tb, "dir": td},
            device_id_type=MESH,
        )

    def ray_copy(kb, kd):
        tb, td = target(kb, kd)
        block = pl.ds(pl.multiple_of(td * rows, rows), rows)
        return pltpu.make_async_remote_copy(
            src_ref=rays_ref.at[:, block, :],
            dst_ref=rays_all.at[me],
            send_sem=ray_send.at[tb * dirs + td],
            recv_sem=ray_recv.at[me],
            device_id={"box": tb, "dir": td},
            device_id_type=MESH,
        )

    for kb, kd in peers:
        parent_copy(kb, kd).start()
    for kb, kd in peers:
        ray_copy(kb, kd).start()

    own = pl.ds(pl.multiple_of(my_dir * rows, rows), rows)
    rays_all[me] = rays_ref[:, own, :]
    parent_all[me] = parent_ref[...]

    lag = lax.broadcasted_iota(jnp.int32, (samples, samples), 1) - lax.broadcasted_iota(
        jnp.int32, (samples, samples), 0
    )

    def add_lag(i, matrix):
        return jnp.where(lag == i, kernel_ref[i], matrix)

    time_matrix = lax.fori_loop(
        0, samples, add_lag, jnp.zeros((samples, samples), jnp.float32)
    )

    def arrived(slot, buffer, sem):
        pltpu.make_async_remote_copy(
            src_ref=buffer.at[slot],
            dst_ref=buffer.at[slot],
            send_sem=sem.at[slot],
            recv_sem=sem.at[slot],
            device_id={"box": my_box, "dir": lax.rem(my_dir + 1, dirs)},
            device_id_type=MESH,
        ).wait_recv()

    for kb, kd in peers:
        sb, sd = target(kb, kd)
        arrived(sb * dirs + sd, parent_all, par_recv)
    parents = jnp.zeros((1, parent_ref.shape[-1]), jnp.float32)
    for slot in range(boxes * dirs):
        parents = parents + parent_all[slot]
    for c in range(top_local):
        match = (lists_ref[:, c : c + 1] == parents).astype(jnp.float32)
        weights_ref[c] = jnp.dot(
            coef_ref[c], match, preferred_element_type=jnp.float32, precision=HIGHEST
        )

    for kb, kd in peers:
        sb, sd = target(kb, kd)
        arrived(sb * dirs + sd, rays_all, ray_recv)

    group = 4 if top_local % 4 == 0 else 1

    def far_group(g, carry):
        base = g * group
        weight = [weights_ref[base + i] for i in range(group)]
        total = [jnp.zeros((rows, samples), jnp.float32) for _ in range(group)]
        for slot in range(boxes * dirs):
            for j in range(runs):
                ray = rays_all[slot, j].astype(jnp.float32)
                at = slot * runs + j
                for i in range(group):
                    total[i] = total[i] + weight[i][:, at : at + 1] * ray
        for i in range(group):
            far_ref[base + i] = total[i]
        return carry

    lax.fori_loop(0, top_local // group, far_group, 0)

    incoming = jnp.dot(
        far_ref[...].reshape(top_local * rows, samples),
        time_matrix,
        preferred_element_type=jnp.float32,
        precision=HIGHEST,
    )
    far_ref[...] = incoming.reshape(top_local, rows, samples)
    first_top = my_box * top_local
    for d in range(dirs):
        held = parent_all[my_box * dirs + d]
        for j in range(runs):
            lane = lax.broadcasted_iota(jnp.int32, held.shape, 1)
            at = (my_box * dirs + d) * runs + j
            parent = jnp.sum(jnp.where(lane == at, held, 0.0), axis=1, keepdims=True)
            chosen = jnp.zeros((rows, samples), jnp.float32)
            for c in range(top_local):
                hit = parent == (first_top + c).astype(jnp.float32)
                chosen = jnp.where(hit, far_ref[c], chosen)
            stage_ref[d, j] = chosen.astype(jnp.bfloat16)

    def back_copy(kd):
        td = lax.rem(my_dir + kd, dirs)
        return pltpu.make_async_remote_copy(
            src_ref=stage_ref.at[td],
            dst_ref=landed.at[my_dir],
            send_sem=back_send.at[td],
            recv_sem=back_recv.at[my_dir],
            device_id={"box": my_box, "dir": td},
            device_id_type=MESH,
        )

    for kd in range(1, dirs):
        back_copy(kd).start()
    landed[my_dir] = stage_ref[my_dir]
    for kb, kd in peers:
        parent_copy(kb, kd).wait_send()
        ray_copy(kb, kd).wait_send()
    for kd in range(1, dirs):
        sd = lax.rem(my_dir + kd, dirs)
        arrived(sd, landed, back_recv)
    for d in range(dirs):
        for j in range(runs):
            out_ref[d * rows : (d + 1) * rows, j * samples : (j + 1) * samples] = landed[d, j]
    for kd in range(1, dirs):
        back_copy(kd).wait_send()


def field_kernel(
    runs,
    chunk,
    blocks_ref,
    maps_ref,
    incoming_ref,
    mask_ref,
    cur_ref,
    before_ref,
    after_ref,
    first_ref,
    last_ref,
    out_ref,
):
    step = pl.program_id(0)
    samples = cur_ref.shape[-1]

    def joined(parts):
        return jnp.concatenate(parts, axis=1)

    lead = joined([jnp.where(step == 0, first_ref[j], before_ref[j, 0]) for j in range(runs)])
    final = step == pl.num_programs(0) - 1
    tail = joined([jnp.where(final, last_ref[j], after_ref[j, 0]) for j in range(runs)])
    pairs = [lead]
    pairs += [joined([cur_ref[j, i] for j in range(runs)]) for i in range(chunk)]
    pairs += [tail]
    dot = functools.partial(jnp.dot, preferred_element_type=jnp.float32)
    for i in range(chunk):
        total = dot(blocks_ref[0], pairs[i + 1]) + dot(maps_ref[i], incoming_ref[...])
        total = total + mask_ref[0, i] * dot(blocks_ref[1], pairs[i])
        total = total + mask_ref[1, i] * dot(blocks_ref[2], pairs[i + 2])
        for j in range(runs):
            out_ref[j, i] = total[:, j * samples : (j + 1) * samples].astype(jnp.bfloat16)


def per_device(
    currents,
    leaf_parent,
    near_links,
    near_blocks,
    aggregate_maps,
    far_boxes,
    far_counts,
    translate_coef,
    time_kernel,
    disaggregate_maps,
):
    boxes, dirs = lax.axis_size("box"), lax.axis_size("dir")
    devices = boxes * dirs
    leaf_count, unknowns, samples = currents.shape
    runs = leaf_count // LEAF_TOP
    top_local, list_slots = far_boxes.shape
    directions = aggregate_maps.shape[1]
    rows = directions // dirs
    box_index, dir_index = lax.axis_index("box"), lax.axis_index("dir")
    me = box_index * dirs + dir_index
    f32, bf16 = jnp.float32, jnp.bfloat16

    chain = [(i, i + 1) for i in range(devices - 1)]
    low = lax.ppermute(currents[-1:], ("box", "dir"), chain)
    high = lax.ppermute(currents[:1], ("box", "dir"), [(b, a) for a, b in chain])
    leaf_runs = currents.reshape(runs, LEAF_TOP, unknowns, samples)

    chunk = 8
    steps = LEAF_TOP // chunk
    matmul_cost = 2 * leaf_count * samples * unknowns * directions
    vmem = pl.BlockSpec(memory_space=pltpu.VMEM)
    rays = pl.pallas_call(
        functools.partial(aggregate_kernel, runs, chunk),
        out_shape=jax.ShapeDtypeStruct((runs, directions, samples), bf16),
        grid=(steps,),
        in_specs=[
            pl.BlockSpec((chunk, directions, unknowns), lambda i: (i, 0, 0)),
            pl.BlockSpec((runs, chunk, unknowns, samples), lambda i: (0, i, 0, 0)),
        ],
        out_specs=pl.BlockSpec((runs, directions, samples), lambda i: (0, 0, 0)),
        scratch_shapes=[pltpu.VMEM((directions, runs * samples), f32)],
        cost_estimate=pl.CostEstimate(
            flops=matmul_cost, bytes_accessed=16 * 2**20, transcendentals=0
        ),
        name="aggregate",
    )(aggregate_maps, leaf_runs)

    total_runs = devices * runs
    width = -(-total_runs // 128) * 128
    run_parent = leaf_parent.reshape(runs, LEAF_TOP)[:, 0].astype(f32)
    lane = jnp.arange(width)
    parent_row = jnp.sum(
        jnp.where(
            lane[None, :] == (me * runs + jnp.arange(runs))[:, None], run_parent[:, None], 0.0
        ),
        axis=0,
    )
    parent_row = jnp.where((lane >= total_runs) & (me == 0), -2.0, parent_row)[None, :]
    is_valid = jnp.arange(list_slots)[None, :] < far_counts[:, None]
    lists = jnp.where(is_valid, far_boxes, -1).astype(f32).T
    coef = lax.dynamic_slice_in_dim(translate_coef, dir_index * rows, rows, 2).transpose(0, 2, 1)
    dma = pltpu.SemaphoreType.DMA
    incoming = pl.pallas_call(
        functools.partial(translate_kernel, boxes, dirs, runs, top_local),
        out_shape=jax.ShapeDtypeStruct((directions, runs * samples), bf16),
        in_specs=[vmem, vmem, vmem, vmem, pl.BlockSpec(memory_space=pltpu.SMEM)],
        out_specs=vmem,
        scratch_shapes=[
            pltpu.VMEM((devices, runs, rows, samples), bf16),
            pltpu.VMEM((devices, 1, width), f32),
            pltpu.VMEM((top_local, rows, width), f32),
            pltpu.VMEM((top_local, rows, samples), f32),
            pltpu.VMEM((dirs, runs, rows, samples), bf16),
            pltpu.VMEM((dirs, runs, rows, samples), bf16),
            dma((devices,)),
            dma((devices,)),
            dma((devices,)),
            dma((devices,)),
            dma((dirs,)),
            dma((dirs,)),
        ],
        compiler_params=pltpu.CompilerParams(collective_id=0, has_side_effects=True),
        name="translate",
    )(rays, parent_row, lists, coef, time_kernel)

    first = jnp.concatenate([low, currents[LEAF_TOP - 1 : -1 : LEAF_TOP]], axis=0)
    last = jnp.concatenate([currents[LEAF_TOP::LEAF_TOP], high], axis=0)
    mask = near_links.astype(f32).reshape(runs, LEAF_TOP, 2).transpose(2, 1, 0)
    mask = jnp.repeat(mask, samples, axis=2)[:, :, None, :]
    near_cost = 4 * matmul_cost
    out = pl.pallas_call(
        functools.partial(field_kernel, runs, chunk),
        out_shape=jax.ShapeDtypeStruct((runs, LEAF_TOP, unknowns, samples), bf16),
        grid=(steps,),
        in_specs=[
            vmem,
            pl.BlockSpec((chunk, unknowns, directions), lambda i: (i, 0, 0)),
            vmem,
            pl.BlockSpec((2, chunk, 1, runs * samples), lambda i: (0, i, 0, 0)),
            pl.BlockSpec((runs, chunk, unknowns, samples), lambda i: (0, i, 0, 0)),
            pl.BlockSpec(
                (runs, 1, unknowns, samples), lambda i: (0, jnp.maximum(i * chunk - 1, 0), 0, 0)
            ),
            pl.BlockSpec(
                (runs, 1, unknowns, samples),
                lambda i: (0, jnp.minimum((i + 1) * chunk, LEAF_TOP - 1), 0, 0),
            ),
            vmem,
            vmem,
        ],
        out_specs=pl.BlockSpec((runs, chunk, unknowns, samples), lambda i: (0, i, 0, 0)),
        cost_estimate=pl.CostEstimate(
            flops=near_cost, bytes_accessed=26 * 2**20, transcendentals=0
        ),
        name="field",
    )(near_blocks, disaggregate_maps, incoming, mask, leaf_runs, leaf_runs, leaf_runs, first, last)
    return out.reshape(leaf_count, unknowns, samples)


def solution(mesh):
    return jax.shard_map(
        per_device,
        mesh=mesh,
        in_specs=(
            P(("box", "dir"), None, None),
            P(("box", "dir")),
            P(("box", "dir"), None),
            P(),
            P(),
            P("box", None),
            P("box"),
            P("box", None, None),
            P(),
            P(),
        ),
        out_specs=P(("box", "dir"), None, None),
        check_vma=False,
    )
```

time: 237 us -> 71.2 us (0.30)
  local copies, waits for them, and re-layouts: 129 us -> 4.7 us
  matrix products: 68.5 us -> 0 us
  Pallas kernels: 0 us -> 57.7 us
  blocking collectives: 21 us -> 0 us
  between operations: 13.6 us -> 0.07 us
  other arithmetic: 1.08 us -> 3.98 us
    gather x1 -> x0, local copies, waits for them, and re-layouts: 97.2 us -> none  [time_matrix(): kernel[jnp.clip(sample_lag, 0, length - 1)]]
    dot_general x12 -> x0, matrix products: 68.5 us -> none  [the longest x1 23.8 us: per_device(): jnp.einsum('pr,lrt->lpt', near_blocks[0], currents, preferred_element_typ...]
    pallas_call x0 -> x3, Pallas kernels: none -> 57.7 us  [the longest x1 32.4 us: per_device(): pl.pallas_call(functools.partial(translate_kernel, boxes, dirs, runs, top...]
    all_gather x1 -> x0, blocking collectives: 21 us -> none  [per_device(): lax.all_gather(own_rays, 'box', axis=1, tiled=True).astype(jnp.float32)]
    slice x4 -> x1, local copies, waits for them, and re-layouts: 19.1 us -> 1.04 us  [per_device(): last = jnp.concatenate([currents[LEAF_TOP::LEAF_TOP], high], axis=0)]
    convert_element_type x2 -> x0, local copies, waits for them, and re-layouts: 11.9 us -> none  [the longest x1 11.9 us: per_device(): return (near_field + far_field).astype(jnp.bfloat16)]
  transfers between devices with their start and end apart: 4 -> 2, of which waited for: 0 -> 0; matrix products, arithmetic and copies ran while one was open for 58% -> 9% of each run, Pallas kernels for 0% -> 60%
where the time goes in v1:
time: 71.2 us; the launch traced here: 70.1 us
  Pallas kernels  57.7 us (81%)
  local copies, waits for them, and re-layouts  4.7 us (7%)
  other arithmetic  3.98 us (6%)
  starting transfers between devices  3.69 us (5%)
    pallas_call x1, Pallas kernels, per_device(): pl.pallas_call(functools.partial(translate_kernel, boxes, dirs, runs, top...  32.4 us
    pallas_call x1, Pallas kernels, per_device(): pl.pallas_call(functools.partial(field_kernel, runs, chunk), out_shape=ja...  15.6 us
    pallas_call x1, Pallas kernels, per_device(): pl.pallas_call(functools.partial(aggregate_kernel, runs, chunk), out_shap...  9.72 us
    ppermute x1, starting transfers between devices, per_device(): low = lax.ppermute(currents[-1:], ('box', 'dir'), chain)  2.4 us
    unnamed x4, local copies, waits for them, and re-layouts  1.68 us
  transfers between devices with their start and end apart: 2, of which 0 were waited for; matrix products, arithmetic and copies ran while one was open for 9% of the time, Pallas kernels for 60%

profile of v1, /device:TPU:0, one launch (start us, length us, event | category | flops | bytes accessed | tf_op | source)
XLA Modules:
  0.0 70.1 jit_solution(8657586891901907221)
XLA Ops:
  0.0 0.0 copy-start
  0.0 1.0 %fusion.1 = (bf16[1,256,128]{2,1,0:T(8,128)(2,1)S(1)}, bf16[1,256,128]{2,1,0:T(8,128)(2,1)S(1)}, bf16[1,256,128]{2,1,0:T(8,128)(2,1)S(1)}, bf16[1,256,128]{2,1,0:T(8,128)(2,1)S(1)}) fusion(bf16[128,256,128]{2,1,0:T(8,128)(2,1)} %param.10), kind=kLoop, calls=%fused_computation.10 | loop fusion | bytes 524288 | tf_op jit(solution)/shard_map/slice | solution.py:333
  1.0 2.4 %collective-permute-start = (bf16[1,256,128]{2,1,0:T(8,128)(2,1)S(1)}, bf16[1,256,128]{2,1,0:T(8,128)(2,1)S(1)}, u32[]{:S(2)}, u32[]{:S(2)}) collective-permute-start(bf16[1,256,128]{2,1,0:T(8,128)(2,1)S(1)} %get-tuple-element.7), channel_id=1, source_target_pairs={{0,1},{1,2},{2,3},{3,4},{4,5},{5,6},{6,7},{7,8},{8,9},{9,10},{10,1... | collective-permute-start | bytes 196616 | tf_op jit(solution)/shard_map/ppermute | solution.py:270
  3.5 1.3 %collective-permute-start.1 = (bf16[1,256,128]{2,1,0:T(8,128)(2,1)S(1)}, bf16[1,256,128]{2,1,0:T(8,128)(2,1)S(1)}, u32[]{:S(2)}, u32[]{:S(2)}) collective-permute-start(bf16[1,256,128]{2,1,0:T(8,128)(2,1)S(1)} %get-tuple-element.8), channel_id=1, source_target_pairs={{1,0},{2,1},{3,2},{4,3},{5,4},{6,5},{7,6},{8,7},{9,8},{10,9},{11,1... | collective-permute-start | bytes 196616 | tf_op jit(solution)/shard_map/ppermute | solution.py:271
  4.8 0.7 %reshape.35 = s32[2,64]{1,0:T(2,128)S(1)} reshape(s32[128]{0:T(128)} %param.11) | data formatting | bytes 1024 | tf_op jit(solution)/shard_map/reshape | solution.py:296
  5.5 0.1 convert_reduce_fusion
  5.6 0.7 convert_element_type.12
  6.3 0.1 reshape.36
  6.4 0.8 %copy.17 = s32[16,64]{0,1:T(8,128)S(1)} copy(s32[16,64]{1,0:T(8,128)} %param.15) | data formatting | bytes 8192 | tf_op args[5]
  7.2 0.1 copy.19
  7.3 0.1 fusion
  7.4 0.5 and_select_fusion.parent_ref
  7.9 1.3 %convert_bitcast_fusion.lists_ref = f32[64,16]{1,0:T(8,128)} fusion(s32[16,64]{0,1:T(8,128)S(1)} %copy.17, s32[16]{0:T(128)} %param.16), kind=kLoop, calls=%fused_computation.2 | loop fusion | flops 3072 | bytes 8256 | tf_op jit(solution)/shard_map/transpose | solution.py:306
  9.1 9.7 %aggregate.1.rays_ref = bf16[2,256,128]{2,1,0:T(8,128)(2,1)} custom-call(bf16[64,256,256]{2,1,0:T(8,128)(2,1)} %maps_ref.2, bf16[2,64,256,128]{3,2,1,0:T(8,128)(2,1)} %bitcast.11), custom_call_target="tpu_custom_call" | custom-call | flops 2147483648 | bytes 16777216 | tf_op jit(solution)/shard_map/aggregate/pallas_call | solution.py:278
  18.9 0.0 copy-done
  18.9 0.2 constant_dynamic-slice_fusion
  19.1 0.9 %copy.20 = f32[16,64,32]{1,2,0:T(8,128)} copy(f32[16,64,32]{2,1,0:T(8,128)S(1)} %constant_dynamic-slice_fusion) | data formatting | bytes 262144
  20.0 32.4 %translate.1.incoming_ref = bf16[256,256]{1,0:T(8,128)(2,1)} custom-call(bf16[2,256,128]{2,1,0:T(8,128)(2,1)} %aggregate.1.rays_ref, f32[1,128]{1,0:T(1,128)} %and_select_fusion.parent_ref, f32[64,16]{1,0:T(8,128)} %convert_bitcast_fusion.lists_ref, f32[16,32,64]{2,1,0:T(8,128)} %bitcast.15, f32[128]{0:T(128)} %kernel_ref.1), custom_call_target="tpu_custom_call" | custom-call | tf_op jit(solution)/shard_map/translate/pallas_call | solution.py:309
  52.3 0.0 collective-permute-done
  52.3 0.7 pad_maximum_fusion.first_ref
  53.0 0.0 collective-permute-done.1
  53.0 0.7 pad_maximum_fusion.1.last_ref
  53.7 0.9 %broadcast_in_dim.36 = f32[2,64,2,128]{3,2,1,0:T(2,128)} broadcast(f32[2,64,2]{2,1,0:T(8,128)S(1)} %copy.19), dimensions={0,1,2} | broadcast | bytes 132096 | tf_op jit(solution)/shard_map/broadcast_in_dim | solution.py:335
  54.5 15.6 %field.1 = bf16[2,64,256,128]{3,2,1,0:T(8,128)(2,1)} custom-call(bf16[3,256,256]{2,1,0:T(8,128)(2,1)} %blocks_ref.1, bf16[64,256,256]{2,1,0:T(8,128)(2,1)} %maps_ref.3, bf16[256,256]{1,0:T(8,128)(2,1)} %translate.1.incoming_ref, f32[2,64,1,256]{3,2,1,0:T(1,128)} %bitcast.16, bf16[2,64,256,128]{3,2,1,0:T(8,128)(2,1)} %bitcast.12, ...), custom_call_target="tpu_custom_call" | custom-call | flops 8589934592 | bytes 27262976 | tf_op jit(solution)/shard_map/field/pallas_call | solution.py:337
  (1 shorter events, 0.0 us)
Async XLA Ops:
  0.0 18.9 %copy-start = (f32[16,64,256]{2,1,0:T(8,128)S(1)}, f32[16,64,256]{2,1,0:T(8,128)}, u32[]{:S(2)}) copy-start(f32[16,64,256]{2,1,0:T(8,128)} %param.17) | copy-start | bytes 3145732
  1.0 51.3 %collective-permute-start = (bf16[1,256,128]{2,1,0:T(8,128)(2,1)S(1)}, bf16[1,256,128]{2,1,0:T(8,128)(2,1)S(1)}, u32[]{:S(2)}, u32[]{:S(2)}) collective-permute-start(bf16[1,256,128]{2,1,0:T(8,128)(2,1)S(1)} %get-tuple-element.7), channel_id=1, source_target_pairs={{0,1},{1,2},{2,3},{3,4},{4,5},{5,6},{6,7},{7,8},{8,9},{9,10},{10,1... | collective-permute-start | bytes 196616 | tf_op jit(solution)/shard_map/ppermute | solution.py:270
  3.5 49.6 %collective-permute-start.1 = (bf16[1,256,128]{2,1,0:T(8,128)(2,1)S(1)}, bf16[1,256,128]{2,1,0:T(8,128)(2,1)S(1)}, u32[]{:S(2)}, u32[]{:S(2)}) collective-permute-start(bf16[1,256,128]{2,1,0:T(8,128)(2,1)S(1)} %get-tuple-element.8), channel_id=1, source_target_pairs={{1,0},{2,1},{3,2},{4,3},{5,4},{6,5},{7,6},{8,7},{9,8},{10,9},{11,1... | collective-permute-start | bytes 196616 | tf_op jit(solution)/shard_map/ppermute | solution.py:271

commit v2 on v1

--- a/solution.py
+++ b/solution.py
@@ -37,11 +37,16 @@
     runs,
     top_local,
     rays_ref,
-    parent_ref,
+    edge_ref,
+    leaf_parent_ref,
     lists_ref,
+    counts_ref,
     coef_ref,
     kernel_ref,
     out_ref,
+    rim_ref,
+    parent_ref,
+    rim,
     rays_all,
     parent_all,
     weights_ref,
@@ -54,12 +59,23 @@
     par_recv,
     back_send,
     back_recv,
+    rim_send,
+    rim_recv,
 ):
     my_box = lax.axis_index("box")
     my_dir = lax.axis_index("dir")
     me = my_box * dirs + my_dir
-    rows = coef_ref.shape[1]
+    devices = boxes * dirs
+    rows = coef_ref.shape[2]
     samples = rays_ref.shape[-1]
+    width = parent_ref.shape[-1]
+    lane = lax.broadcasted_iota(jnp.int32, (1, width), 1)
+    spare = jnp.where(me == 0, -1, 0)
+    parent_row = jnp.where(lane >= devices * runs, spare, jnp.zeros((1, width), jnp.int32))
+    for j in range(runs):
+        parent_row = jnp.where(lane == me * runs + j, leaf_parent_ref[j * LEAF_TOP], parent_row)
+    parent_ref[...] = parent_row.astype(jnp.float32)
+    rim[...] = jnp.zeros_like(rim)
     peers = [(kb, kd) for kb in range(boxes) for kd in range(dirs) if kb or kd]
     peers.sort(key=lambda p: -min(p[0], boxes - p[0]))
 
@@ -97,10 +113,29 @@
             device_id_type=MESH,
         )
 
+    def rim_copy(side):
+        other = lax.rem(me + (1 if side == 0 else devices - 1), devices)
+        return pltpu.make_async_remote_copy(
+            src_ref=edge_ref.at[side],
+            dst_ref=rim.at[side],
+            send_sem=rim_send.at[side],
+            recv_sem=rim_recv.at[side],
+            device_id={"box": lax.div(other, dirs), "dir": lax.rem(other, dirs)},
+            device_id_type=MESH,
+        )
+
     for kb, kd in peers:
         parent_copy(kb, kd).start()
     for kb, kd in peers:
         ray_copy(kb, kd).start()
+
+    @pl.when(me < devices - 1)
+    def _():
+        rim_copy(0).start()
+
+    @pl.when(me > 0)
+    def _():
+        rim_copy(1).start()
 
     own = pl.ds(pl.multiple_of(my_dir * rows, rows), rows)
     rays_all[me] = rays_ref[:, own, :]
@@ -130,13 +165,21 @@
     for kb, kd in peers:
         sb, sd = target(kb, kd)
         arrived(sb * dirs + sd, parent_all, par_recv)
-    parents = jnp.zeros((1, parent_ref.shape[-1]), jnp.float32)
-    for slot in range(boxes * dirs):
+    parents = jnp.zeros((1, width), jnp.float32)
+    for slot in range(devices):
         parents = parents + parent_all[slot]
+    slots = lists_ref.shape[1]
+    column = jnp.broadcast_to(parents, (128, width)).T[:, :slots]
+    spot = lax.broadcasted_iota(jnp.int32, (1, slots), 1)
     for c in range(top_local):
-        match = (lists_ref[:, c : c + 1] == parents).astype(jnp.float32)
-        weights_ref[c] = jnp.dot(
-            coef_ref[c], match, preferred_element_type=jnp.float32, precision=HIGHEST
+        used = jnp.where(spot < counts_ref[c], lists_ref[c : c + 1, :], -2)
+        match = (column == used.astype(jnp.float32)).astype(jnp.float32)
+        weights_ref[c] = lax.dot_general(
+            coef_ref[c],
+            match,
+            (((0,), (1,)), ((), ())),
+            preferred_element_type=jnp.float32,
+            precision=HIGHEST,
         )
 
     for kb, kd in peers:
@@ -172,7 +215,6 @@
     for d in range(dirs):
         held = parent_all[my_box * dirs + d]
         for j in range(runs):
-            lane = lax.broadcasted_iota(jnp.int32, held.shape, 1)
             at = (my_box * dirs + d) * runs + j
             parent = jnp.sum(jnp.where(lane == at, held, 0.0), axis=1, keepdims=True)
             chosen = jnp.zeros((rows, samples), jnp.float32)
@@ -198,6 +240,18 @@
     for kb, kd in peers:
         parent_copy(kb, kd).wait_send()
         ray_copy(kb, kd).wait_send()
+
+    @pl.when(me < devices - 1)
+    def _():
+        rim_copy(0).wait_send()
+        rim_copy(1).wait_recv()
+
+    @pl.when(me > 0)
+    def _():
+        rim_copy(1).wait_send()
+        rim_copy(0).wait_recv()
+
+    rim_ref[...] = rim[...]
     for kd in range(1, dirs):
         sd = lax.rem(my_dir + kd, dirs)
         arrived(sd, landed, back_recv)
@@ -209,38 +263,37 @@
 
 
 def field_kernel(
-    runs,
-    chunk,
-    blocks_ref,
-    maps_ref,
-    incoming_ref,
-    mask_ref,
-    cur_ref,
-    before_ref,
-    after_ref,
-    first_ref,
-    last_ref,
-    out_ref,
+    runs, chunk, blocks_ref, maps_ref, incoming_ref, links_ref, cur_ref, rim_ref, out_ref
 ):
     step = pl.program_id(0)
     samples = cur_ref.shape[-1]
+    first = step * chunk
+    dot = functools.partial(jnp.dot, preferred_element_type=jnp.float32)
 
     def joined(parts):
         return jnp.concatenate(parts, axis=1)
 
-    lead = joined([jnp.where(step == 0, first_ref[j], before_ref[j, 0]) for j in range(runs)])
+    before = jnp.maximum(first - 1, 0)
+    after = jnp.minimum(first + chunk, LEAF_TOP - 1)
     final = step == pl.num_programs(0) - 1
-    tail = joined([jnp.where(final, last_ref[j], after_ref[j, 0]) for j in range(runs)])
-    pairs = [lead]
-    pairs += [joined([cur_ref[j, i] for j in range(runs)]) for i in range(chunk)]
-    pairs += [tail]
-    dot = functools.partial(jnp.dot, preferred_element_type=jnp.float32)
+    lead = [rim_ref[0]] + [cur_ref[j, LEAF_TOP - 1] for j in range(runs - 1)]
+    tail = [cur_ref[j, 0] for j in range(1, runs)] + [rim_ref[1]]
+    lead = [jnp.where(step == 0, lead[j], cur_ref[j, before]) for j in range(runs)]
+    tail = [jnp.where(final, tail[j], cur_ref[j, after]) for j in range(runs)]
+    pairs = [joined(lead)]
+    pairs += [joined([cur_ref[j, first + i] for j in range(runs)]) for i in range(chunk)]
+    pairs += [joined(tail)]
     for i in range(chunk):
-        total = dot(blocks_ref[0], pairs[i + 1]) + dot(maps_ref[i], incoming_ref[...])
-        total = total + mask_ref[0, i] * dot(blocks_ref[1], pairs[i])
-        total = total + mask_ref[1, i] * dot(blocks_ref[2], pairs[i + 2])
+        at = first + i
+        total = dot(blocks_ref[0], pairs[i + 1]) + dot(maps_ref[at], incoming_ref[...])
+        low = dot(blocks_ref[1], pairs[i])
+        high = dot(blocks_ref[2], pairs[i + 2])
         for j in range(runs):
-            out_ref[j, i] = total[:, j * samples : (j + 1) * samples].astype(jnp.bfloat16)
+            span = slice(j * samples, (j + 1) * samples)
+            with_low = links_ref[0, j * LEAF_TOP + at].astype(jnp.float32)
+            with_high = links_ref[1, j * LEAF_TOP + at].astype(jnp.float32)
+            part = total[:, span] + with_low * low[:, span] + with_high * high[:, span]
+            out_ref[j, i] = part.astype(jnp.bfloat16)
 
 
 def per_device(
@@ -262,13 +315,9 @@
     top_local, list_slots = far_boxes.shape
     directions = aggregate_maps.shape[1]
     rows = directions // dirs
-    box_index, dir_index = lax.axis_index("box"), lax.axis_index("dir")
-    me = box_index * dirs + dir_index
+    dir_index = lax.axis_index("dir")
     f32, bf16 = jnp.float32, jnp.bfloat16
 
-    chain = [(i, i + 1) for i in range(devices - 1)]
-    low = lax.ppermute(currents[-1:], ("box", "dir"), chain)
-    high = lax.ppermute(currents[:1], ("box", "dir"), [(b, a) for a, b in chain])
     leaf_runs = currents.reshape(runs, LEAF_TOP, unknowns, samples)
 
     chunk = 8
@@ -293,25 +342,21 @@
 
     total_runs = devices * runs
     width = -(-total_runs // 128) * 128
-    run_parent = leaf_parent.reshape(runs, LEAF_TOP)[:, 0].astype(f32)
-    lane = jnp.arange(width)
-    parent_row = jnp.sum(
-        jnp.where(
-            lane[None, :] == (me * runs + jnp.arange(runs))[:, None], run_parent[:, None], 0.0
-        ),
-        axis=0,
-    )
-    parent_row = jnp.where((lane >= total_runs) & (me == 0), -2.0, parent_row)[None, :]
-    is_valid = jnp.arange(list_slots)[None, :] < far_counts[:, None]
-    lists = jnp.where(is_valid, far_boxes, -1).astype(f32).T
-    coef = lax.dynamic_slice_in_dim(translate_coef, dir_index * rows, rows, 2).transpose(0, 2, 1)
+    coef = lax.dynamic_slice_in_dim(translate_coef, dir_index * rows, rows, 2)
+    edges = jnp.stack([currents[-1], currents[0]])
+    smem = pl.BlockSpec(memory_space=pltpu.SMEM)
     dma = pltpu.SemaphoreType.DMA
-    incoming = pl.pallas_call(
+    incoming, rim = pl.pallas_call(
         functools.partial(translate_kernel, boxes, dirs, runs, top_local),
-        out_shape=jax.ShapeDtypeStruct((directions, runs * samples), bf16),
-        in_specs=[vmem, vmem, vmem, vmem, pl.BlockSpec(memory_space=pltpu.SMEM)],
-        out_specs=vmem,
+        out_shape=(
+            jax.ShapeDtypeStruct((directions, runs * samples), bf16),
+            jax.ShapeDtypeStruct((2, unknowns, samples), bf16),
+        ),
+        in_specs=[vmem, vmem, smem, vmem, smem, vmem, smem],
+        out_specs=(vmem, vmem),
         scratch_shapes=[
+            pltpu.VMEM((1, width), f32),
+            pltpu.VMEM((2, unknowns, samples), bf16),
             pltpu.VMEM((devices, runs, rows, samples), bf16),
             pltpu.VMEM((devices, 1, width), f32),
             pltpu.VMEM((top_local, rows, width), f32),
@@ -324,42 +369,31 @@
             dma((devices,)),
             dma((dirs,)),
             dma((dirs,)),
+            dma((2,)),
+            dma((2,)),
         ],
-        compiler_params=pltpu.CompilerParams(collective_id=0, has_side_effects=True),
+        compiler_params=pltpu.CompilerParams(
+            collective_id=0, has_side_effects=True, vmem_limit_bytes=16 * 2**20
+        ),
+        cost_estimate=pl.CostEstimate(
+            flops=8 * matmul_cost, bytes_accessed=2 * 2**20, transcendentals=0
+        ),
         name="translate",
-    )(rays, parent_row, lists, coef, time_kernel)
-
-    first = jnp.concatenate([low, currents[LEAF_TOP - 1 : -1 : LEAF_TOP]], axis=0)
-    last = jnp.concatenate([currents[LEAF_TOP::LEAF_TOP], high], axis=0)
-    mask = near_links.astype(f32).reshape(runs, LEAF_TOP, 2).transpose(2, 1, 0)
-    mask = jnp.repeat(mask, samples, axis=2)[:, :, None, :]
+    )(rays, edges, leaf_parent, far_boxes, far_counts, coef, time_kernel)
+
     near_cost = 4 * matmul_cost
     out = pl.pallas_call(
         functools.partial(field_kernel, runs, chunk),
         out_shape=jax.ShapeDtypeStruct((runs, LEAF_TOP, unknowns, samples), bf16),
         grid=(steps,),
-        in_specs=[
-            vmem,
-            pl.BlockSpec((chunk, unknowns, directions), lambda i: (i, 0, 0)),
-            vmem,
-            pl.BlockSpec((2, chunk, 1, runs * samples), lambda i: (0, i, 0, 0)),
-            pl.BlockSpec((runs, chunk, unknowns, samples), lambda i: (0, i, 0, 0)),
-            pl.BlockSpec(
-                (runs, 1, unknowns, samples), lambda i: (0, jnp.maximum(i * chunk - 1, 0), 0, 0)
-            ),
-            pl.BlockSpec(
-                (runs, 1, unknowns, samples),
-                lambda i: (0, jnp.minimum((i + 1) * chunk, LEAF_TOP - 1), 0, 0),
-            ),
-            vmem,
-            vmem,
-        ],
+        in_specs=[vmem, vmem, vmem, smem, vmem, vmem],
         out_specs=pl.BlockSpec((runs, chunk, unknowns, samples), lambda i: (0, i, 0, 0)),
         cost_estimate=pl.CostEstimate(
             flops=near_cost, bytes_accessed=26 * 2**20, transcendentals=0
         ),
         name="field",
-    )(near_blocks, disaggregate_maps, incoming, mask, leaf_runs, leaf_runs, leaf_runs, first, last)
+        compiler_params=pltpu.CompilerParams(vmem_limit_bytes=12 * 2**20),
+    )(near_blocks, disaggregate_maps, incoming, near_links.T, leaf_runs, rim)
     return out.reshape(leaf_count, unknowns, samples)
 
 

time: 71.2 us -> 54.1 us (0.76)
  Pallas kernels: 57.7 us -> 51 us
  other arithmetic: 3.98 us -> 0.02 us
  starting transfers between devices: 3.69 us -> 0 us
  local copies, waits for them, and re-layouts: 4.7 us -> 2.18 us
    ppermute x2 -> x0, starting transfers between devices: 3.69 us -> none  [the longest x1 2.4 us: per_device(): low = lax.ppermute(currents[-1:], ('box', 'dir'), chain)]
    pallas_call x1, Pallas kernels: 15.6 us -> 12 us  [per_device(): pl.pallas_call(functools.partial(field_kernel, runs, chunk), out_shape=ja...]
    pallas_call x1, Pallas kernels: 32.4 us -> 29.2 us  [per_device(): pl.pallas_call(functools.partial(translate_kernel, boxes, dirs, runs, top...]
    concatenate x2 -> x0, other arithmetic: 1.34 us -> none  [the longest x1 0.67 us: per_device(): first = jnp.concatenate([low, currents[LEAF_TOP - 1:-1:LEAF_TOP]], axis=0)]
    transpose x1 -> x0, other arithmetic: 1.26 us -> none  [per_device(): lists = jnp.where(is_valid, far_boxes, -1).astype(f32).T]
    broadcast_in_dim x1 -> x0, local copies, waits for them, and re-layouts: 0.85 us -> none  [per_device(): mask = jnp.repeat(mask, samples, axis=2)[:, :, None, :]]
    reshape x2 -> x0, local copies, waits for them, and re-layouts: 0.82 us -> none  [the longest x1 0.74 us: per_device(): run_parent = leaf_parent.reshape(runs, LEAF_TOP)[:, 0].astype(f32)]
    convert_element_type x2 -> x0, other arithmetic: 0.8 us -> none  [the longest x1 0.68 us: per_device(): mask = near_links.astype(f32).reshape(runs, LEAF_TOP, 2).transpose(2, 1, 0)]
  transfers between devices with their start and end apart: 2 -> 0, of which waited for: 0 -> 0; matrix products, arithmetic and copies ran while one was open for 9% -> 0% of each run, Pallas kernels for 60% -> 0%
where the time goes in v2:
time: 54.1 us; the launch traced here: 53.3 us
  Pallas kernels  51 us (94%)
  local copies, waits for them, and re-layouts  2.18 us (4%)
    pallas_call x1, Pallas kernels, per_device(): pl.pallas_call(functools.partial(translate_kernel, boxes, dirs, runs, top...  29.2 us
    pallas_call x1, Pallas kernels, per_device(): pl.pallas_call(functools.partial(field_kernel, runs, chunk), out_shape=ja...  12 us
    pallas_call x1, Pallas kernels, per_device(): pl.pallas_call(functools.partial(aggregate_kernel, runs, chunk), out_shap...  9.82 us
    unnamed x22, local copies, waits for them, and re-layouts  1.09 us

profile of v2, /device:TPU:0, one launch (start us, length us, event | category | flops | bytes accessed | tf_op | source)
XLA Modules:
  0.0 53.3 jit_solution(12324544211489487901)
XLA Ops:
  0.0 0.0 copy-start
  0.0 0.0 copy-start.4
  0.0 0.0 copy-start.6
  0.0 0.0 copy-start.7
  0.0 0.0 copy-start.8
  0.0 9.8 %aggregate.1.rays_ref = bf16[2,256,128]{2,1,0:T(8,128)(2,1)} custom-call(bf16[64,256,256]{2,1,0:T(8,128)(2,1)} %maps_ref.2, bf16[2,64,256,128]{3,2,1,0:T(8,128)(2,1)} %bitcast.3), custom_call_target="tpu_custom_call" | custom-call | flops 2147483648 | bytes 16777216 | tf_op jit(solution)/shard_map/aggregate/pallas_call | solution.py:327
  9.8 0.9 %fusion = (bf16[1,256,128]{2,1,0:T(8,128)(2,1)S(1)}, bf16[1,256,128]{2,1,0:T(8,128)(2,1)S(1)}) fusion(bf16[128,256,128]{2,1,0:T(8,128)(2,1)} %param.10), kind=kLoop, calls=%fused_computation.2 | loop fusion | bytes 262144 | tf_op jit(solution)/shard_map/slice | solution.py:346
  10.7 0.0 copy-done
  10.8 0.0 slice-start
  10.8 0.2 constant_dynamic-slice_fusion.coef_ref
  11.0 0.0 copy-done.4
  11.0 0.0 copy-done.6
  11.0 0.0 copy-done.7
  11.0 0.0 copy-done.8
  11.0 0.0 copy-start.1
  11.0 1.0 %copy-done.1 = bf16[2,256,128]{2,1,0:T(8,128)(2,1)S(1)} copy-done((bf16[2,256,128]{2,1,0:T(8,128)(2,1)S(1)}, bf16[2,256,128]{2,1,0:T(8,128)(2,1)}, u32[]{:S(2)}) %copy-start.1) | copy-done | bytes 131096
  12.1 0.0 slice-start.1
  12.1 0.0 copy-start.2
  12.1 0.0 copy-start.3
  12.1 0.0 copy-start.5
  12.1 29.2 %translate.1 = (bf16[256,256]{1,0:T(8,128)(2,1)S(1)}, bf16[2,256,128]{2,1,0:T(8,128)(2,1)S(1)}) custom-call(bf16[2,256,128]{2,1,0:T(8,128)(2,1)S(1)} %copy-done.1, bf16[2,256,128]{2,1,0:T(8,128)(2,1)S(1)} %pad_maximum_fusion.edge_ref, s32[128]{0:T(128)S(1)} %copy-done.6, s32[16,64]{1,0:T(8,128)S(1)} %copy-done.4, s32[16]{0:T(128)S(1)} %copy-done.7, ...), custom_call_target="tpu_custom_call" | custom-call | flops 17179869184 | bytes 2097152 | tf_op jit(solution)/shard_map/translate/pallas_call | solution.py:349
  41.3 0.0 slice-done
  41.3 0.0 slice-done.1
  41.3 0.0 copy-done.2
  41.3 0.0 copy-done.3
  41.3 0.0 copy-done.5
  41.3 12.0 %field.1 = bf16[2,64,256,128]{3,2,1,0:T(8,128)(2,1)} custom-call(bf16[3,256,256]{2,1,0:T(8,128)(2,1)S(1)} %copy-done.3, bf16[64,256,256]{2,1,0:T(8,128)(2,1)S(1)} %copy-done.2, bf16[256,256]{1,0:T(8,128)(2,1)S(1)} %get-tuple-element.7.incoming_ref, s32[2,128]{1,0:T(2,128)S(1)} %bitcast.7, bf16[2,64,256,128]{3,2,1,0:T(8,128)(2,1)S(1)} %bitcast.6, ...), custom_call_target="tpu_custom_call" | custom-call | flops 8589934592 | bytes 27262976 | tf_op jit(solution)/shard_map/field/pallas_call | solution.py:385
  (2 shorter events, 0.0 us)
Async XLA Ops:
  0.0 10.8 %copy-start = (f32[16,64,256]{2,1,0:T(8,128)S(1)}, f32[16,64,256]{2,1,0:T(8,128)}, u32[]{:S(2)}) copy-start(f32[16,64,256]{2,1,0:T(8,128)} %param.17) | copy-start | bytes 3145732
  0.0 11.0 %copy-start.4 = (s32[16,64]{1,0:T(8,128)S(1)}, s32[16,64]{1,0:T(8,128)}, u32[]{:S(2)}) copy-start(s32[16,64]{1,0:T(8,128)} %lists_ref.1) | copy-start | bytes 12292
  0.0 11.0 %copy-start.6 = (s32[128]{0:T(128)S(1)}, s32[128]{0:T(128)}, u32[]{:S(2)}) copy-start(s32[128]{0:T(128)} %leaf_parent_ref.1) | copy-start | bytes 1540
  0.0 11.0 %copy-start.7 = (s32[16]{0:T(128)S(1)}, s32[16]{0:T(128)}, u32[]{:S(2)}) copy-start(s32[16]{0:T(128)} %counts_ref.1) | copy-start | bytes 196
  0.0 11.0 %copy-start.8 = (f32[128]{0:T(128)S(1)}, f32[128]{0:T(128)}, u32[]{:S(2)}) copy-start(f32[128]{0:T(128)} %kernel_ref.1) | copy-start | bytes 1540
  10.8 30.5 %slice-start = ((s8[8388608]{0:T(1024)(128)(4,1)}), s8[4194304]{0:T(1024)(128)(4,1)S(1)}, s32[]{:S(2)}) async-start(s8[8388608]{0:T(1024)(128)(4,1)} %bitcast.4), calls=%async_computation | async-start | bytes 8388608
  11.0 1.1 %copy-start.1 = (bf16[2,256,128]{2,1,0:T(8,128)(2,1)S(1)}, bf16[2,256,128]{2,1,0:T(8,128)(2,1)}, u32[]{:S(2)}) copy-start(bf16[2,256,128]{2,1,0:T(8,128)(2,1)} %aggregate.1.rays_ref) | copy-start | bytes 393220
  12.1 29.2 %slice-start.1 = ((s8[8388608]{0:T(1024)(128)(4,1)}), s8[4194304]{0:T(1024)(128)(4,1)S(1)}, s32[]{:S(2)}) async-start(s8[8388608]{0:T(1024)(128)(4,1)} %bitcast.4), calls=%async_computation.1 | async-start | bytes 8388608
  12.1 29.2 %copy-start.2 = (bf16[64,256,256]{2,1,0:T(8,128)(2,1)S(1)}, bf16[64,256,256]{2,1,0:T(8,128)(2,1)}, u32[]{:S(2)}) copy-start(bf16[64,256,256]{2,1,0:T(8,128)(2,1)} %maps_ref.3) | copy-start | bytes 25165828
  12.1 29.2 %copy-start.3 = (bf16[3,256,256]{2,1,0:T(8,128)(2,1)S(1)}, bf16[3,256,256]{2,1,0:T(8,128)(2,1)}, u32[]{:S(2)}) copy-start(bf16[3,256,256]{2,1,0:T(8,128)(2,1)} %blocks_ref.1) | copy-start | bytes 1179652
  12.1 29.2 %copy-start.5 = (s32[128,2]{0,1:T(2,128)S(1)}, s32[128,2]{0,1:T(2,128)}, u32[]{:S(2)}) copy-start(s32[128,2]{0,1:T(2,128)} %param.12) | copy-start | bytes 3076

commit v3 on v2

--- a/solution.py
+++ b/solution.py
@@ -11,22 +11,23 @@
 HIGHEST = lax.Precision.HIGHEST
 
 
-def aggregate_kernel(runs, chunk, maps_ref, cur_ref, out_ref, acc_ref):
+def aggregate_kernel(runs, chunk, maps_ref, cur_ref, out_ref, edge_ref, acc_ref):
     step = pl.program_id(0)
     samples = cur_ref.shape[-1]
 
     @pl.when(step == 0)
     def _():
         acc_ref[...] = jnp.zeros_like(acc_ref)
-
-    total = acc_ref[...]
-    for i in range(chunk):
-        pair = jnp.concatenate([cur_ref[j, i] for j in range(runs)], axis=1)
-        total = total + jnp.dot(maps_ref[i], pair, preferred_element_type=jnp.float32)
-    acc_ref[...] = total
+        edge_ref[1] = cur_ref[0, 0]
+
+    maps = jnp.concatenate([maps_ref[i] for i in range(chunk)], axis=1)
+    depth = chunk * cur_ref.shape[2]
+    leaves = jnp.concatenate([cur_ref[j].reshape(depth, samples) for j in range(runs)], axis=1)
+    acc_ref[...] += jnp.dot(maps, leaves, preferred_element_type=jnp.float32)
 
     @pl.when(step == pl.num_programs(0) - 1)
     def _():
+        edge_ref[0] = cur_ref[runs - 1, chunk - 1]
         for j in range(runs):
             out_ref[j] = acc_ref[:, j * samples : (j + 1) * samples].astype(jnp.bfloat16)
 
@@ -280,20 +281,23 @@
     tail = [cur_ref[j, 0] for j in range(1, runs)] + [rim_ref[1]]
     lead = [jnp.where(step == 0, lead[j], cur_ref[j, before]) for j in range(runs)]
     tail = [jnp.where(final, tail[j], cur_ref[j, after]) for j in range(runs)]
+    spans = [slice(j * samples, (j + 1) * samples) for j in range(runs)]
     pairs = [joined(lead)]
     pairs += [joined([cur_ref[j, first + i] for j in range(runs)]) for i in range(chunk)]
     pairs += [joined(tail)]
     for i in range(chunk):
         at = first + i
-        total = dot(blocks_ref[0], pairs[i + 1]) + dot(maps_ref[at], incoming_ref[...])
-        low = dot(blocks_ref[1], pairs[i])
-        high = dot(blocks_ref[2], pairs[i + 2])
+        low = [pairs[i][:, span] for span in spans]
+        high = [pairs[i + 2][:, span] for span in spans]
         for j in range(runs):
-            span = slice(j * samples, (j + 1) * samples)
-            with_low = links_ref[0, j * LEAF_TOP + at].astype(jnp.float32)
-            with_high = links_ref[1, j * LEAF_TOP + at].astype(jnp.float32)
-            part = total[:, span] + with_low * low[:, span] + with_high * high[:, span]
-            out_ref[j, i] = part.astype(jnp.bfloat16)
+            leaf = j * LEAF_TOP + at
+            low[j] = jnp.where(links_ref[0, leaf] != 0, low[j], jnp.zeros_like(low[j]))
+            high[j] = jnp.where(links_ref[1, leaf] != 0, high[j], jnp.zeros_like(high[j]))
+        left = joined([blocks_ref[0], blocks_ref[1], blocks_ref[2], maps_ref[at]])
+        right = [pairs[i + 1], joined(low), joined(high), incoming_ref[...]]
+        total = dot(left, jnp.concatenate(right, axis=0))
+        for j in range(runs):
+            out_ref[j, i] = total[:, spans[j]].astype(jnp.bfloat16)
 
 
 def per_device(
@@ -324,15 +328,22 @@
     steps = LEAF_TOP // chunk
     matmul_cost = 2 * leaf_count * samples * unknowns * directions
     vmem = pl.BlockSpec(memory_space=pltpu.VMEM)
-    rays = pl.pallas_call(
+    rays, edges = pl.pallas_call(
         functools.partial(aggregate_kernel, runs, chunk),
-        out_shape=jax.ShapeDtypeStruct((runs, directions, samples), bf16),
+        out_shape=(
+            jax.ShapeDtypeStruct((runs, directions, samples), bf16),
+            jax.ShapeDtypeStruct((2, unknowns, samples), bf16),
+        ),
         grid=(steps,),
         in_specs=[
             pl.BlockSpec((chunk, directions, unknowns), lambda i: (i, 0, 0)),
             pl.BlockSpec((runs, chunk, unknowns, samples), lambda i: (0, i, 0, 0)),
         ],
-        out_specs=pl.BlockSpec((runs, directions, samples), lambda i: (0, 0, 0)),
+        out_specs=(
+            pl.BlockSpec((runs, directions, samples), lambda i: (0, 0, 0)),
+            pl.BlockSpec((2, unknowns, samples), lambda i: (0, 0, 0)),
+        ),
+        compiler_params=pltpu.CompilerParams(vmem_limit_bytes=58 * 2**20),
         scratch_shapes=[pltpu.VMEM((directions, runs * samples), f32)],
         cost_estimate=pl.CostEstimate(
             flops=matmul_cost, bytes_accessed=16 * 2**20, transcendentals=0
@@ -343,7 +354,6 @@
     total_runs = devices * runs
     width = -(-total_runs // 128) * 128
     coef = lax.dynamic_slice_in_dim(translate_coef, dir_index * rows, rows, 2)
-    edges = jnp.stack([currents[-1], currents[0]])
     smem = pl.BlockSpec(memory_space=pltpu.SMEM)
     dma = pltpu.SemaphoreType.DMA
     incoming, rim = pl.pallas_call(
@@ -352,7 +362,7 @@
             jax.ShapeDtypeStruct((directions, runs * samples), bf16),
             jax.ShapeDtypeStruct((2, unknowns, samples), bf16),
         ),
-        in_specs=[vmem, vmem, smem, vmem, smem, vmem, smem],
+        in_specs=[vmem, pl.BlockSpec(memory_space=pl.ANY), smem, vmem, smem, vmem, smem],
         out_specs=(vmem, vmem),
         scratch_shapes=[
             pltpu.VMEM((1, width), f32),

time: 54.1 us -> 54.6 us (level)
  local copies, waits for them, and re-layouts: 2.18 us -> 2.83 us
    unnamed x22 -> x26, local copies, waits for them, and re-layouts: 1.09 us -> 2.62 us
    slice x1 -> x0, local copies, waits for them, and re-layouts: 0.88 us -> none  [per_device(): edges = jnp.stack([currents[-1], currents[0]])]
where the time goes in v3:
time: 54.6 us; the launch traced here: 53.9 us
  Pallas kernels  51 us (93%)
  local copies, waits for them, and re-layouts  2.83 us (5%)
    pallas_call x1, Pallas kernels, per_device(): pl.pallas_call(functools.partial(translate_kernel, boxes, dirs, runs, top...  29.2 us
    pallas_call x1, Pallas kernels, per_device(): pl.pallas_call(functools.partial(field_kernel, runs, chunk), out_shape=ja...  11.9 us
    pallas_call x1, Pallas kernels, per_device(): pl.pallas_call(functools.partial(aggregate_kernel, runs, chunk), out_shap...  9.89 us
    unnamed x26, local copies, waits for them, and re-layouts  2.62 us

profile of v3, /device:TPU:0, one launch (start us, length us, event | category | flops | bytes accessed | tf_op | source)
XLA Modules:
  0.0 53.9 jit_solution(3498206082064095525)
XLA Ops:
  0.0 0.0 copy-start
  0.0 0.0 copy-start.4
  0.0 0.0 copy-start.6
  0.0 0.0 copy-start.7
  0.0 0.0 copy-start.8
  0.0 9.9 %aggregate.1 = (bf16[2,256,128]{2,1,0:T(8,128)(2,1)}, bf16[2,256,128]{2,1,0:T(8,128)(2,1)}) custom-call(bf16[64,256,256]{2,1,0:T(8,128)(2,1)} %maps_ref.2, bf16[2,64,256,128]{3,2,1,0:T(8,128)(2,1)} %bitcast.3), custom_call_target="tpu_custom_call" | custom-call | flops 2147483648 | bytes 16777216 | tf_op jit(solution)/shard_map/aggregate/pallas_call | solution.py:331
  9.9 0.0 copy-done
  9.9 0.0 slice-start
  9.9 0.0 slice-start.2
  9.9 0.2 constant_dynamic-slice_fusion.coef_ref
  10.1 0.0 copy-done.4
  10.1 0.0 copy-done.6
  10.2 0.0 copy-done.7
  10.2 0.0 copy-done.8
  10.2 0.0 copy-start.2
  10.2 1.0 %copy-done.2 = bf16[2,256,128]{2,1,0:T(8,128)(2,1)S(1)} copy-done((bf16[2,256,128]{2,1,0:T(8,128)(2,1)S(1)}, bf16[2,256,128]{2,1,0:T(8,128)(2,1)}, u32[]{:S(2)}) %copy-start.2) | copy-done | bytes 131096
  11.2 0.0 copy-start.3
  11.2 1.5 %copy-done.3 = bf16[2,256,128]{2,1,0:T(8,128)(2,1)S(1)} copy-done((bf16[2,256,128]{2,1,0:T(8,128)(2,1)S(1)}, bf16[2,256,128]{2,1,0:T(8,128)(2,1)}, u32[]{:S(2)}) %copy-start.3) | copy-done | bytes 131096
  12.8 0.0 slice-start.1
  12.8 0.0 slice-start.3
  12.8 0.0 copy-start.1
  12.8 0.0 copy-start.5
  12.8 29.2 %translate.1 = (bf16[256,256]{1,0:T(8,128)(2,1)S(1)}, bf16[2,256,128]{2,1,0:T(8,128)(2,1)S(1)}) custom-call(bf16[2,256,128]{2,1,0:T(8,128)(2,1)S(1)} %copy-done.2, bf16[2,256,128]{2,1,0:T(8,128)(2,1)S(1)} %copy-done.3, s32[128]{0:T(128)S(1)} %copy-done.6, s32[16,64]{1,0:T(8,128)S(1)} %copy-done.4, s32[16]{0:T(128)S(1)} %copy-done.7, ...), custom_call_target="tpu_custom_call" | custom-call | flops 17179869184 | bytes 2097152 | tf_op jit(solution)/shard_map/translate/pallas_call | solution.py:359
  42.0 0.0 slice-done
  42.0 0.0 slice-done.2
  42.0 0.0 slice-done.1
  42.0 0.0 slice-done.3
  42.0 0.0 copy-done.1
  42.0 0.0 copy-done.5
  42.0 11.9 %field.1 = bf16[2,64,256,128]{3,2,1,0:T(8,128)(2,1)} custom-call(bf16[3,256,256]{2,1,0:T(8,128)(2,1)S(1)} %copy-done.1, bf16[64,256,256]{2,1,0:T(8,128)(2,1)S(1)} %bitcast.8, bf16[256,256]{1,0:T(8,128)(2,1)S(1)} %get-tuple-element.11.incoming_ref, s32[2,128]{1,0:T(2,128)S(1)} %bitcast.9, bf16[2,64,256,128]{3,2,1,0:T(8,128)(2,1)S(1)} %bitcast.6, ...), custom_call_target="tpu_custom_call" | custom-call | flops 8589934592 | bytes 27262976 | tf_op jit(solution)/shard_map/field/pallas_call | solution.py:395
  (2 shorter events, 0.0 us)
Async XLA Ops:
  0.0 9.9 %copy-start = (f32[16,64,256]{2,1,0:T(8,128)S(1)}, f32[16,64,256]{2,1,0:T(8,128)}, u32[]{:S(2)}) copy-start(f32[16,64,256]{2,1,0:T(8,128)} %param.17) | copy-start | bytes 3145732
  0.0 10.1 %copy-start.4 = (s32[16,64]{1,0:T(8,128)S(1)}, s32[16,64]{1,0:T(8,128)}, u32[]{:S(2)}) copy-start(s32[16,64]{1,0:T(8,128)} %lists_ref.1) | copy-start | bytes 12292
  0.0 10.1 %copy-start.6 = (s32[128]{0:T(128)S(1)}, s32[128]{0:T(128)}, u32[]{:S(2)}) copy-start(s32[128]{0:T(128)} %leaf_parent_ref.1) | copy-start | bytes 1540
  0.0 10.2 %copy-start.7 = (s32[16]{0:T(128)S(1)}, s32[16]{0:T(128)}, u32[]{:S(2)}) copy-start(s32[16]{0:T(128)} %counts_ref.1) | copy-start | bytes 196
  0.0 10.2 %copy-start.8 = (f32[128]{0:T(128)S(1)}, f32[128]{0:T(128)}, u32[]{:S(2)}) copy-start(f32[128]{0:T(128)} %kernel_ref.1) | copy-start | bytes 1540
  9.9 32.0 %slice-start = ((s8[8388608]{0:T(1024)(128)(4,1)}), s8[4194304]{0:T(1024)(128)(4,1)S(1)}, s32[]{:S(2)}) async-start(s8[8388608]{0:T(1024)(128)(4,1)} %bitcast.4), calls=%async_computation | async-start | bytes 8388608
  9.9 32.0 %slice-start.2 = ((s8[8388608]{0:T(1024)(128)(4,1)}), s8[4194304]{0:T(1024)(128)(4,1)S(1)}, s32[]{:S(2)}) async-start(s8[8388608]{0:T(1024)(128)(4,1)} %bitcast.7), calls=%async_computation.2 | async-start | bytes 8388608
  10.2 1.1 %copy-start.2 = (bf16[2,256,128]{2,1,0:T(8,128)(2,1)S(1)}, bf16[2,256,128]{2,1,0:T(8,128)(2,1)}, u32[]{:S(2)}) copy-start(bf16[2,256,128]{2,1,0:T(8,128)(2,1)} %get-tuple-element.9.rays_ref) | copy-start | bytes 393220
  11.2 1.5 %copy-start.3 = (bf16[2,256,128]{2,1,0:T(8,128)(2,1)S(1)}, bf16[2,256,128]{2,1,0:T(8,128)(2,1)}, u32[]{:S(2)}) copy-start(bf16[2,256,128]{2,1,0:T(8,128)(2,1)} %get-tuple-element.10.edge_ref) | copy-start | bytes 393220
  12.8 29.2 %slice-start.1 = ((s8[8388608]{0:T(1024)(128)(4,1)}), s8[4194304]{0:T(1024)(128)(4,1)S(1)}, s32[]{:S(2)}) async-start(s8[8388608]{0:T(1024)(128)(4,1)} %bitcast.4), calls=%async_computation.1 | async-start | bytes 8388608
  12.8 29.2 %slice-start.3 = ((s8[8388608]{0:T(1024)(128)(4,1)}), s8[4194304]{0:T(1024)(128)(4,1)S(1)}, s32[]{:S(2)}) async-start(s8[8388608]{0:T(1024)(128)(4,1)} %bitcast.7), calls=%async_computation.3 | async-start | bytes 8388608
  12.8 29.2 %copy-start.1 = (bf16[3,256,256]{2,1,0:T(8,128)(2,1)S(1)}, bf16[3,256,256]{2,1,0:T(8,128)(2,1)}, u32[]{:S(2)}) copy-start(bf16[3,256,256]{2,1,0:T(8,128)(2,1)} %blocks_ref.1) | copy-start | bytes 1179652
  12.8 29.2 %copy-start.5 = (s32[128,2]{0,1:T(2,128)S(1)}, s32[128,2]{0,1:T(2,128)}, u32[]{:S(2)}) copy-start(s32[128,2]{0,1:T(2,128)} %param.12) | copy-start | bytes 3076
